TPU v7x, 256 devices: a whole 4x4x8 slice. The times are simulated.
256 devices in a mesh: row: 32 (over x, z_hi, core), col: 8 (over z_lo, y).
Axes of the slice: x: 4, y: 4, z: 8 (z_hi: 4, z_lo: 2; z = z_hi * 2 + z_lo), core: 2. Of those that a mesh axis runs over, the one named last changes fastest.
Arguments:
- amplitudes: float32 [32, 8, 1024, 1024], P('row', 'col'), may hold values from -6 to 6
- panels_left: bfloat16 [32, 2, 1024, 1024], P('row', None, 'col'), may hold values from -6 to 6
- panels_right: bfloat16 [8, 2, 1024, 1024], P('col', None, 'row'), may hold values from -6 to 6
- weights_right: bfloat16 [2, 8, 1024, 1024], P(None, 'col', 'row'), may hold values from -0.125 to 0.125
- weights_left: bfloat16 [2, 32, 1024, 1024], P(None, 'row', 'col'), may hold values from -0.125 to 0.125
- energy_left: float32 [32], P('row'), may hold values from -2 to -0.5
- energy_right: float32 [8], P('col'), may hold values from -2 to -0.5
- energy_virtual: float32 [1024], replicated, may hold values from 0.5 to 3
Outputs:
- updated: float32 [32, 8, 1024, 1024], P('row', 'col')
All inputs are finite; a program needn't handle non-finite values.
Results may differ from a plain program's by a relative error of at most 0.0018.
Values may be sent and summed in bfloat16 or wider, within the bound.
A program may use at most 128 MiB of HBM per device.

v0:
```python
import jax
import jax.numpy as jnp
from jax import lax
from jax.sharding import PartitionSpec as P


def combine_blocks(blocks):
    as_float = blocks.astype(jnp.float32)
    return (2.0 * as_float - jnp.swapaxes(as_float, -1, -2)).astype(jnp.bfloat16)


def body(
    amplitudes,
    panels_left,
    panels_right,
    weights_right,
    weights_left,
    energy_left,
    energy_right,
    energy_virtual,
):
    left_slab = panels_left[0]
    right_slab = panels_right[0]
    right_weight_slab = weights_right[:, 0]
    left_weight_slab = weights_left[:, 0]
    left_whole = lax.all_gather(left_slab, "col", axis=1, tiled=True)
    left_mixed = combine_blocks(left_whole)
    mixed_cols = left_mixed
    direct = jnp.einsum(
        "kac,kcb->ab",
        mixed_cols,
        lax.all_gather(right_weight_slab, "row", axis=1, tiled=True),
        preferred_element_type=jnp.float32,
    )
    right_whole = lax.all_gather(right_slab, "row", axis=1, tiled=True)
    right_mixed = combine_blocks(right_whole)
    mixed_cols = right_mixed
    mirror = jnp.einsum(
        "kac,kcb->ab",
        mixed_cols,
        lax.all_gather(left_weight_slab, "col", axis=1, tiled=True),
        preferred_element_type=jnp.float32,
    )
    residual = direct + jnp.transpose(mirror)
    virt_pair = energy_virtual[:, None] + energy_virtual[None, :]
    denominator = energy_left[0] + energy_right[0] - virt_pair
    return (amplitudes[0, 0] + residual / denominator)[None, None]


def solution(mesh):
    placed = (
        P("row", "col", None, None),
        P("row", None, "col", None),
        P("col", None, "row", None),
        P(None, "col", "row", None),
        P(None, "row", "col", None),
        P("row"),
        P("col"),
        P(),
    )
    return jax.shard_map(
        body, mesh=mesh, in_specs=placed, out_specs=P("row", "col", None, None), check_vma=False
    )
```

profile of v0, /device:TPU:1, one launch (start us, length us, event | category | flops | bytes accessed | tf_op | source)
XLA Modules:
  0.0 267.6 jit_solution(162221997629663721)
XLA Ops:
  6.5 0.0 all-gather.9.cloned.1.call-start
  6.5 0.7 all-gather.9.cloned.1.call-update
  7.3 0.0 all-gather.13.cloned.1.call-start
  7.3 0.7 all-gather.13.cloned.1.call-update
  8.0 0.0 all-gather.11.cloned.1.call-start
  8.1 0.7 all-gather.11.cloned.1.call-update
  8.7 0.0 all-gather.15.cloned.1.call-start
  8.8 0.5 all-gather.15.cloned.1.call-update
  10.6 57.3 %all-gather.9.cloned.1.call-done = bf16[1,2,1024,1024]{3,2,1,0:T(8,128)(2,1)} async-done(((bf16[1,2,128,1024]{3,2,1,0:T(8,128)(2,1)}), bf16[1,2,1024,1024]{3,2,1,0:T(8,128)(2,1)}) %all-gather.9.cloned.1.call-update) | async-done | bytes 4194320 | tf_op jit(solution)/shard_map/all_gather | solution.py:26
  68.0 6.5 %bitcast_convert_fusion.1 = f32[2,1024,1024]{2,1,0:T(8,128)} fusion(bf16[1,2,1024,1024]{3,2,1,0:T(8,128)(2,1)} %all-gather.9.cloned.1.call-done), kind=kLoop, calls=%fused_computation.13 | loop fusion | flops 2097152 | bytes 12582912 | tf_op jit(solution)/shard_map/convert_element_type | solution.py:8
  74.4 8.7 %copy.9 = f32[2,1024,1024]{1,2,0:T(8,128)} copy(f32[2,1024,1024]{2,1,0:T(8,128)} %bitcast_convert_fusion.1) | data formatting | bytes 16777216 | tf_op jit(solution)/shard_map/convert_element_type | solution.py:8
  83.1 47.2 %all-gather.13.cloned.1.call-done = bf16[1,2,1024,1024]{3,2,1,0:T(8,128)(2,1)} async-done(((bf16[1,2,32,1024]{3,2,1,0:T(8,128)(2,1)}), bf16[1,2,1024,1024]{3,2,1,0:T(8,128)(2,1)}) %all-gather.13.cloned.1.call-update) | async-done | bytes 4194320 | tf_op jit(solution)/shard_map/all_gather | solution.py:35
  130.2 6.5 %bitcast_convert_fusion = f32[2,1024,1024]{2,1,0:T(8,128)} fusion(bf16[1,2,1024,1024]{3,2,1,0:T(8,128)(2,1)} %all-gather.13.cloned.1.call-done), kind=kLoop, calls=%fused_computation.11 | loop fusion | flops 2097152 | bytes 12582912 | tf_op jit(solution)/shard_map/convert_element_type | solution.py:8
  136.7 8.7 %copy.12 = f32[2,1024,1024]{1,2,0:T(8,128)} copy(f32[2,1024,1024]{2,1,0:T(8,128)} %bitcast_convert_fusion) | data formatting | bytes 16777216 | tf_op jit(solution)/shard_map/convert_element_type | solution.py:8
  145.4 0.0 copy-start
  145.4 45.9 %all-gather.11.cloned.1.call-done = bf16[2,1,1024,1024]{3,2,0,1:T(8,128)(2,1)} async-done(((bf16[2,1,32,1024]{3,2,0,1:T(8,128)(2,1)}), bf16[2,1,1024,1024]{3,2,0,1:T(8,128)(2,1)}) %all-gather.11.cloned.1.call-update) | async-done | bytes 4194320 | tf_op jit(solution)/shard_map/all_gather | solution.py:32
  191.4 12.6 %fusion.2 = f32[1024,1024,1]{1,0,2:T(8,128)} fusion(f32[2,1024,1024]{1,2,0:T(8,128)} %copy.9, bf16[2,1,1024,1024]{3,2,0,1:T(8,128)(2,1)} %all-gather.11.cloned.1.call-done, bf16[1,2,1024,1024]{3,2,1,0:T(8,128)(2,1)} %all-gather.9.cloned.1.call-done), kind=kOutput, calls=%fused_computation.4 | convolution fusion | flops 4303355904 | bytes 20971520 | tf_op jit(solution)/shard_map/kac,kcb->ab/dot_general | solution.py:29
  204.0 41.8 %all-gather.15.cloned.1.call-done = bf16[2,1,1024,1024]{3,2,0,1:T(8,128)(2,1)} async-done(((bf16[2,1,128,1024]{3,2,0,1:T(8,128)(2,1)}), bf16[2,1,1024,1024]{3,2,0,1:T(8,128)(2,1)}) %all-gather.15.cloned.1.call-update) | async-done | bytes 4194320 | tf_op jit(solution)/shard_map/all_gather | solution.py:41
  245.8 0.0 copy-done
  245.8 15.3 %fusion.8 = f32[1,1,1024,1024]{3,2,1,0:T(8,128)} fusion(f32[1024,1024,1]{1,0,2:T(8,128)} %fusion.2, f32[1,1,1024,1024]{3,2,1,0:T(8,128)} %param.8, f32[1024]{0:T(1024)S(1)} %copy-done, f32[]{:T(128)} %bitcast.14, bf16[2,1,1024,1024]{3,2,0,1:T(8,128)(2,1)} %all-gather.15.cloned.1.call-done, f32[2,1024,1024]{1,2,0:T(8,128)} %copy.12, ...), kind=kOutput, calls=%fused_computation.9 | convolution fusion | flops 4308598784 | bytes 29364228 | tf_op jit(solution)/shard_map/kac,kcb->ab/dot_general | solution.py:38
Async XLA Ops:
  6.5 61.4 %all-gather.9.cloned.1.call-start = ((), (), s32[]{:S(2)}) async-start(), calls=%async_computation | async-start | bytes 4718592 | tf_op jit(solution)/shard_map/all_gather | solution.py:26
  7.3 123.0 %all-gather.13.cloned.1.call-start = ((), (), s32[]{:S(2)}) async-start(), calls=%async_computation.2 | async-start | bytes 4325376 | tf_op jit(solution)/shard_map/all_gather | solution.py:35
  8.0 183.4 %all-gather.11.cloned.1.call-start = ((), (), s32[]{:S(2)}) async-start(), calls=%async_computation.1 | async-start | bytes 4325376 | tf_op jit(solution)/shard_map/all_gather | solution.py:32
  8.7 237.0 %all-gather.15.cloned.1.call-start = ((), (), s32[]{:S(2)}) async-start(), calls=%async_computation.3 | async-start | bytes 4718592 | tf_op jit(solution)/shard_map/all_gather | solution.py:41
  145.4 100.3 %copy-start = (f32[1024]{0:T(1024)S(1)}, f32[1024]{0:T(1024)}, u32[]{:S(2)}) copy-start(f32[1024]{0:T(1024)} %param.15) | copy-start | bytes 12292
Sparse Core Ops, SparseCore 0:
  9.1 58.7 all-gather.8
  70.6 59.5 all-gather.12
  132.9 58.4 all-gather.10
  193.0 52.7 all-gather.14
where the time goes:
time: 268 us
  waiting for transfers between devices  195 us (73%)
  matrix products  27.9 us (10%)
  local copies, waits for them, and re-layouts  17.4 us (6%)
  between operations  14.4 us (5%)
  other arithmetic  12.9 us (5%)
    all_gather x1, waiting for transfers between devices, body(): left_whole = lax.all_gather(left_slab, 'col', axis=1, tiled=True)  57.3 us
    all_gather x1, waiting for transfers between devices, body(): right_whole = lax.all_gather(right_slab, 'row', axis=1, tiled=True)  47.2 us
    all_gather x1, waiting for transfers between devices, body(): lax.all_gather(right_weight_slab, 'row', axis=1, tiled=True)  45.9 us
    all_gather x1, waiting for transfers between devices, body(): lax.all_gather(left_weight_slab, 'col', axis=1, tiled=True)  41.8 us
    convert_element_type x2, local copies, waits for them, and re-layouts, combine_blocks(): as_float = blocks.astype(jnp.float32)  17.4 us
    dot_general x1, matrix products, body(): jnp.einsum('kac,kcb->ab', mixed_cols, lax.all_gather(left_weight_slab, 'c...  15.3 us
    convert_element_type x2, other arithmetic, combine_blocks(): as_float = blocks.astype(jnp.float32)  12.9 us
    dot_general x1, matrix products, body(): jnp.einsum('kac,kcb->ab', mixed_cols, lax.all_gather(right_weight_slab, '...  12.6 us
  transfers between devices with their start and end apart: 4, of which 4 were waited for; matrix products, arithmetic and copies ran while one was open for 16% of the time, Pallas kernels for 0%

commit v1 on v0

v1 whole, which is shorter than its diff:
```python
import jax
import jax.numpy as jnp
from jax import lax
from jax.experimental import pallas as pl
from jax.experimental.pallas import tpu as pltpu
from jax.sharding import PartitionSpec as P

MESH = pl.DeviceIdType.MESH
F32 = jnp.float32
BF16 = jnp.bfloat16
N_MSG = 64


def gather_kernel(panl, panr, wtr, wtl, out, awi, awj, lm, rmt, wt, lsem, ssem, rsem):
    row, col = lax.axis_index("row"), lax.axis_index("col")
    x, zh, core = row // 8, lax.rem(row // 2, 4), lax.rem(row, 2)
    zl, y = col // 4, lax.rem(col, 4)

    def at_x(d):
        return lax.rem(x + d + 4, 4)

    def at_z(d):
        return lax.rem(zh + d + 4, 4)

    def at_y(d):
        return lax.rem(y + d + 4, 4)

    def row_of(x_, zh_, core_):
        return (x_ * 4 + zh_) * 2 + core_

    dev = {
        "x+": (row_of(at_x(1), zh, core), col),
        "x-": (row_of(at_x(-1), zh, core), col),
        "z+": (row_of(x, at_z(1), core), col),
        "z-": (row_of(x, at_z(-1), core), col),
        "y+": (row, zl * 4 + at_y(1)),
        "y-": (row, zl * 4 + at_y(-1)),
        "zi": (row, (1 - zl) * 4 + y),
        "core": (row_of(x, zh, 1 - core), col),
    }

    own = [
        pltpu.make_async_copy(panl, awi.at[0:2, col], lsem.at[0]),
        pltpu.make_async_copy(panr, awj.at[0:2, x, zh, core], lsem.at[1]),
        pltpu.make_async_copy(wtr, awj.at[2:4, x, zh, core], lsem.at[2]),
        pltpu.make_async_copy(wtl, awi.at[2:4, col], lsem.at[3]),
    ]
    for copy in own:
        copy.start()

    barrier = pltpu.get_barrier_semaphore()
    for peer in dev.values():
        pl.semaphore_signal(barrier, inc=1, device_id=peer, device_id_type=MESH)
    pl.semaphore_wait(barrier, len(dev))
    for copy in own:
        copy.wait()

    ids = {}
    sent = []

    def describe(name, ref, to):
        number = ids.setdefault(name, len(ids))
        return pltpu.make_async_remote_copy(
            src_ref=ref, dst_ref=ref, send_sem=ssem.at[number], recv_sem=rsem.at[number],
            device_id=dev[to], device_id_type=MESH,
        )

    def send(name, ref, to):
        copy = describe(name, ref, to)
        copy.start()
        sent.append(copy)

    def got(name, ref):
        describe(name, ref, "core").wait_recv()

    def j(dx, dz, lo=0, hi=4):
        return awj.at[lo:hi, at_x(dx), at_z(dz), core]

    def i(part, dy, same=True, lo=0, hi=128):
        return awi.at[part, (zl if same else 1 - zl) * 4 + at_y(dy), lo:hi]

    A0, A1, W0, W1 = 0, 1, 2, 3
    OPP = {"+": "-", "-": "+"}
    STEP = {"+": 1, "-": -1}

    def ring_send(tag, part, same, signs="+-"):
        for s in signs:
            send(f"{tag}{part}{s}", i(part, 0, same), "y" + s)

    def ring_got(tag, part, same, s):
        got(f"{tag}{part}{s}", i(part, -STEP[s], same))

    def ring_forward(tag, part, same, s, lo=0, hi=128):
        send(f"{tag}f{part}{s}", i(part, -STEP[s], same, lo, hi), "y" + s)

    def ring_got_forward(tag, part, same, s, lo=0, hi=128):
        got(f"{tag}f{part}{s}", i(part, 2, same, lo, hi))

    def x_send(dz):
        for s in "+-":
            send(f"x{dz}{s}", j(0, dz), "x" + s)

    def x_forward(dz):
        for s in "+-":
            got(f"x{dz}{s}", j(-STEP[s], dz))
        send(f"xf{dz}+", j(-1, dz, 0, 2), "x+")
        send(f"xf{dz}-", j(1, dz, 2, 4), "x-")

    def x_got_forward(dz):
        got(f"xf{dz}+", j(2, dz, 0, 2))
        got(f"xf{dz}-", j(2, dz, 2, 4))

    def share(dx):
        send(f"core{dx}", awj.at[:, at_x(dx), :, core], "core")

    def got_share(dx):
        got(f"core{dx}", awj.at[:, at_x(dx), :, 1 - core])

    def mix_left(blk):
        start = pl.multiple_of(blk * 128, 128)

        def one(k, _):
            for h in range(2):
                cols = slice(h * 512, h * 512 + 512)
                straight = awi[k, blk, :, cols].astype(F32)
                turned = awi[k, h * 4:h * 4 + 4, :, pl.ds(start, 128)].reshape(512, 128).T.astype(F32)
                lm[k, pl.ds(start, 128), cols] = (2.0 * straight - turned).astype(BF16)
            return _

        lax.fori_loop(0, 2, one, 0)

    def mix_right(blk):
        start = pl.multiple_of(blk * 128, 128)

        def one(k, _):
            for h in range(2):
                cols = slice(h * 512, h * 512 + 512)
                straight = awj[k, blk // 2, pl.ds(lax.rem(blk, 2) * 2, 2), :, :, cols].reshape(128, 512).astype(F32)
                turned = awj[k, h * 2:h * 2 + 2, :, :, :, pl.ds(start, 128)].reshape(512, 128).T.astype(F32)
                rmt[blk, pl.ds(pl.multiple_of(k * 128, 128), 128), cols] = (2.0 * turned - straight).astype(BF16)
            return _

        lax.fori_loop(0, 2, one, 0)

    def direct_tile(m):
        rows = pl.ds(pl.multiple_of(m * 256, 256), 256)

        def one(n, _):
            cols = pl.ds(pl.multiple_of(n * 256, 256), 256)
            total = jnp.zeros((256, 256), F32)
            for k in range(2):
                total += jnp.dot(lm[k, rows, :], awj[2 + k, :, :, :, :, cols].reshape(1024, 256),
                                 preferred_element_type=F32)
            out[rows, cols] = total
            return _

        lax.fori_loop(0, 4, one, 0)

    def mirror_slot(slot):
        for k in range(2):
            for h in range(2):
                cols = slice(h * 512, h * 512 + 512)
                wt[cols, k * 128:k * 128 + 128] = awi[2 + k, slot, :, cols].T

        def one(n, _):
            cols = pl.ds(pl.multiple_of(n * 256, 256), 256)
            out[:, cols] += jnp.dot(wt[...], rmt[slot, :, cols], preferred_element_type=F32)
            return _

        lax.fori_loop(0, 4, one, 0)

    def loop(count, task):
        def one(n, _):
            task(n)
            return _
        lax.fori_loop(0, count, one, 0)

    def slot_of(dy, same):
        return (zl if same else 1 - zl) * 4 + at_y(dy)

    send("jz+", j(0, 0), "z+")
    send("jz-", j(0, 0), "z-")
    ring_send("y", A0, True)
    ring_send("y", A1, True)
    x_send(0)
    send("zA0", i(A0, 0), "zi")
    send("zA1", i(A1, 0), "zi")
    ring_send("y", W1, True)
    send("zW0", i(W0, 0), "zi")
    send("zW1.0", i(W1, 0), "zi")

    x_forward(0)
    got("jz+", j(0, -1))
    got("jz-", j(0, 1))
    send("jzf+", j(0, -1, 0, 2), "z+")
    send("jzf-", j(0, 1, 2, 4), "z-")
    x_send(-1)
    x_send(1)
    ring_got("y", A0, True, "+")
    ring_forward("y", A0, True, "+")
    ring_got("y", A1, True, "-")
    ring_forward("y", A1, True, "-")
    got("zA0", i(A0, 0, False))
    ring_send("p", A0, False)
    got("zA1", i(A1, 0, False))
    ring_send("p", A1, False)
    got("jzf+", j(0, 2, 0, 2))
    got("jzf-", j(0, 2, 2, 4))
    x_send(2)
    share(0)
    x_got_forward(0)
    x_forward(-1)
    x_forward(1)
    ring_got("y", W1, True, "+")
    ring_got("y", W1, True, "-")
    send("zW1.-", i(W1, -1), "zi")
    send("zW1.+", i(W1, 1), "zi")
    ring_got("y", A0, True, "-")
    ring_got("y", A1, True, "+")
    ring_got_forward("y", A0, True, "+")
    ring_got_forward("y", A1, True, "-")
    ring_got("p", A0, False, "+")
    ring_forward("p", A0, False, "+")
    ring_got("p", A1, False, "-")
    ring_forward("p", A1, False, "-")
    ring_forward("y", W1, True, "+", 0, 64)
    ring_forward("y", W1, True, "-", 64, 128)
    ring_send("y", W0, True)
    got("zW0", i(W0, 0, False))
    ring_send("p", W0, False)
    x_forward(2)
    x_got_forward(-1)
    x_got_forward(1)
    x_got_forward(2)
    for dx in (-1, 1, 2):
        share(dx)
    ring_got_forward("y", W1, True, "+", 0, 64)
    ring_got_forward("y", W1, True, "-", 64, 128)
    send("zW1.2", i(W1, 2), "zi")
    ring_got("p", A0, False, "-")
    ring_got("p", A1, False, "+")
    ring_got_forward("p", A0, False, "+")
    ring_got_forward("p", A1, False, "-")
    loop(8, mix_left)
    for dx in (0, -1, 1, 2):
        got_share(dx)
    loop(8, mix_right)
    ring_got("y", W0, True, "+")
    ring_got("y", W0, True, "-")
    ring_forward("y", W0, True, "+", 0, 64)
    ring_forward("y", W0, True, "-", 64, 128)
    loop(4, direct_tile)
    mirror_slot(slot_of(0, True))
    ring_got("p", W0, False, "+")
    ring_got("p", W0, False, "-")
    ring_forward("p", W0, False, "+", 0, 64)
    ring_forward("p", W0, False, "-", 64, 128)
    mirror_slot(slot_of(-1, True))
    mirror_slot(slot_of(1, True))
    got("zW1.0", i(W1, 0, False))
    mirror_slot(slot_of(0, False))
    got("zW1.-", i(W1, -1, False))
    mirror_slot(slot_of(-1, False))
    got("zW1.+", i(W1, 1, False))
    mirror_slot(slot_of(1, False))
    ring_got_forward("y", W0, True, "+", 0, 64)
    ring_got_forward("y", W0, True, "-", 64, 128)
    mirror_slot(slot_of(2, True))
    got("zW1.2", i(W1, 2, False))
    ring_got_forward("p", W0, False, "+", 0, 64)
    ring_got_forward("p", W0, False, "-", 64, 128)
    mirror_slot(slot_of(2, False))
    for copy in sent:
        copy.wait_send()
    assert len(ids) <= N_MSG


def body(amplitudes, panels_left, panels_right, weights_right, weights_left, energy_left, energy_right, energy_virtual):
    residual = pl.pallas_call(
        gather_kernel,
        out_shape=jax.ShapeDtypeStruct((1024, 1024), F32),
        in_specs=[pl.BlockSpec(memory_space=pl.ANY)] * 4,
        out_specs=pl.BlockSpec(memory_space=pltpu.VMEM),
        scratch_shapes=[
            pltpu.VMEM((4, 8, 128, 1024), BF16),
            pltpu.VMEM((4, 4, 4, 2, 32, 1024), BF16),
            pltpu.VMEM((2, 1024, 1024), BF16),
            pltpu.VMEM((8, 256, 1024), BF16),
            pltpu.VMEM((1024, 256), BF16),
            pltpu.SemaphoreType.DMA((4,)),
            pltpu.SemaphoreType.DMA((N_MSG,)),
            pltpu.SemaphoreType.DMA((N_MSG,)),
        ],
        compiler_params=pltpu.CompilerParams(
            collective_id=0, has_side_effects=True, vmem_limit_bytes=44 * 1024 * 1024
        ),
        name="gather_products",
    )(panels_left[0], panels_right[0], weights_right[:, 0], weights_left[:, 0])
    virt_pair = energy_virtual[:, None] + energy_virtual[None, :]
    denominator = energy_left[0] + energy_right[0] - virt_pair
    return (amplitudes[0, 0] + residual / denominator)[None, None]


def solution(mesh):
    placed = (
        P("row", "col", None, None),
        P("row", None, "col", None),
        P("col", None, "row", None),
        P(None, "col", "row", None),
        P(None, "row", "col", None),
        P("row"),
        P("col"),
        P(),
    )
    return jax.shard_map(
        body, mesh=mesh, in_specs=placed, out_specs=P("row", "col", None, None), check_vma=False
    )
```

time: 268 us -> 104 us (0.39)
  waiting for transfers between devices: 195 us -> 0 us
  Pallas kernels: 0 us -> 95.6 us
  matrix products: 27.9 us -> 0 us
  local copies, waits for them, and re-layouts: 17.4 us -> 3.89 us
  between operations: 14.4 us -> 1.35 us
  other arithmetic: 12.9 us -> 2.77 us
    all_gather x4 -> x0, waiting for transfers between devices: 192 us -> none  [the longest x1 57.3 us: body(): left_whole = lax.all_gather(left_slab, 'col', axis=1, tiled=True)]
    pallas_call x0 -> x1, Pallas kernels: none -> 95.6 us  [body(): pl.pallas_call(gather_kernel, out_shape=jax.ShapeDtypeStruct((1024, 1024)...]
    dot_general x2 -> x0, matrix products: 27.9 us -> none  [the longest x1 15.3 us: body(): jnp.einsum('kac,kcb->ab', mixed_cols, lax.all_gather(left_weight_slab, 'c...]
    convert_element_type x2 -> x0, local copies, waits for them, and re-layouts: 17.4 us -> none  [combine_blocks(): as_float = blocks.astype(jnp.float32)]
    convert_element_type x2 -> x0, other arithmetic: 12.9 us -> none  [combine_blocks(): as_float = blocks.astype(jnp.float32)]
    unnamed x2 -> x12, local copies, waits for them, and re-layouts: 0.01 us -> 3.89 us
    broadcast_in_dim x0 -> x1, other arithmetic: none -> 2.77 us  [body(): return (amplitudes[0, 0] + residual / denominator)[None, None]]
  transfers between devices with their start and end apart: 4 -> 0, of which waited for: 4 -> 0; matrix products, arithmetic and copies ran while one was open for 16% -> 0% of each run, Pallas kernels for 0% -> 0%
where the time goes in v1:
time: 104 us
  Pallas kernels  95.6 us (92%)
  local copies, waits for them, and re-layouts  3.89 us (4%)
  other arithmetic  2.77 us (3%)
  between operations  1.35 us (1%)
    pallas_call x1, Pallas kernels, body(): pl.pallas_call(gather_kernel, out_shape=jax.ShapeDtypeStruct((1024, 1024)...  95.6 us
    unnamed x12, local copies, waits for them, and re-layouts  3.89 us
    broadcast_in_dim x1, other arithmetic, body(): return (amplitudes[0, 0] + residual / denominator)[None, None]  2.77 us

profile of v1, /device:TPU:1, one launch (start us, length us, event | category | flops | bytes accessed | tf_op | source)
XLA Modules:
  0.0 103.6 jit_solution(7358818805359310461)
XLA Ops:
  0.0 0.0 copy-start.5
  1.3 0.0 copy-start
  1.3 1.0 copy-done
  2.4 0.0 copy-start.1
  2.4 1.0 %copy-done.1 = bf16[2,1,128,1024]{3,2,1,0:T(8,128)(2,1)S(1)} copy-done((bf16[2,1,128,1024]{3,2,1,0:T(8,128)(2,1)S(1)}, bf16[2,1,128,1024]{3,2,1,0:T(8,128)(2,1)}, u32[]{:S(2)}) %copy-start.1) | copy-done | bytes 524312
  3.4 0.0 copy-start.2
  3.4 0.9 copy-done.2
  4.3 0.0 copy-start.3
  4.3 0.9 copy-done.3
  5.2 0.0 copy-start.4
  5.2 95.6 %gather_products.1 = f32[1024,1024]{1,0:T(8,128)S(1)} custom-call(bf16[2,128,1024]{2,1,0:T(8,128)(2,1)S(1)} %bitcast.11, bf16[2,32,1024]{2,1,0:T(8,128)(2,1)S(1)} %bitcast.13, bf16[2,32,1024]{2,1,0:T(8,128)(2,1)S(1)} %bitcast.14, bf16[2,128,1024]{2,1,0:T(8,128)(2,1)S(1)} %bitcast.12), custom_call_target="tpu_custom_call" | custom-call | tf_op jit(solution)/shard_map/gather_products/pallas_call | solution.py:279
  100.8 0.0 copy-done.5
  100.9 0.0 copy-done.4
  100.9 2.8 %fusion = f32[1,1,1024,1024]{3,2,1,0:T(8,128)} fusion(f32[1,1,1024,1024]{3,2,1,0:T(8,128)S(1)} %copy-done.4, f32[1024,1024]{1,0:T(8,128)S(1)} %gather_products.1, f32[1024]{0:T(1024)S(1)} %copy-done.5, f32[]{:T(128)} %bitcast.5), kind=kLoop, calls=%fused_computation.1 | loop fusion | flops 4194304 | bytes 12587012 | tf_op jit(solution)/shard_map/broadcast_in_dim | solution.py:301
Async XLA Ops:
  0.0 100.8 %copy-start.5 = (f32[1024]{0:T(1024)S(1)}, f32[1024]{0:T(1024)}, u32[]{:S(2)}) copy-start(f32[1024]{0:T(1024)} %param.15) | copy-start | bytes 12292
  1.3 1.0 %copy-start = (bf16[1,2,128,1024]{3,2,1,0:T(8,128)(2,1)S(1)}, bf16[1,2,128,1024]{3,2,1,0:T(8,128)(2,1)}, u32[]{:S(2)}) copy-start(bf16[1,2,128,1024]{3,2,1,0:T(8,128)(2,1)} %param.9) | copy-start | bytes 1572868
  2.4 1.0 %copy-start.1 = (bf16[2,1,128,1024]{3,2,1,0:T(8,128)(2,1)S(1)}, bf16[2,1,128,1024]{3,2,1,0:T(8,128)(2,1)}, u32[]{:S(2)}) copy-start(bf16[2,1,128,1024]{3,2,1,0:T(8,128)(2,1)} %param.12) | copy-start | bytes 1572868
  3.4 0.9 copy-start.2
  4.3 0.9 copy-start.3
  5.2 95.6 %copy-start.4 = (f32[1,1,1024,1024]{3,2,1,0:T(8,128)S(1)}, f32[1,1,1024,1024]{3,2,1,0:T(8,128)}, u32[]{:S(2)}) copy-start(f32[1,1,1024,1024]{3,2,1,0:T(8,128)} %param.8) | copy-start | bytes 12582916

commit v2 on v1

--- a/solution.py
+++ b/solution.py
@@ -8,10 +8,11 @@
 MESH = pl.DeviceIdType.MESH
 F32 = jnp.float32
 BF16 = jnp.bfloat16
-N_MSG = 64
-
-
-def gather_kernel(panl, panr, wtr, wtl, out, awi, awj, lm, rmt, wt, lsem, ssem, rsem):
+N_MSG = 56
+
+
+def gather_kernel(panl, panr, wtr, wtl, amp_in, ev_in, el, er, out, awi, awj, lm, rmt, wt, amp, inv, ev,
+                  lsem, ssem, rsem):
     row, col = lax.axis_index("row"), lax.axis_index("col")
     x, zh, core = row // 8, lax.rem(row // 2, 4), lax.rem(row, 2)
     zl, y = col // 4, lax.rem(col, 4)
@@ -45,7 +46,11 @@
         pltpu.make_async_copy(wtr, awj.at[2:4, x, zh, core], lsem.at[2]),
         pltpu.make_async_copy(wtl, awi.at[2:4, col], lsem.at[3]),
     ]
-    for copy in own:
+    small = [
+        pltpu.make_async_copy(ev_in, ev, lsem.at[4]),
+    ]
+    load = pltpu.make_async_copy(amp_in, amp, lsem.at[5])
+    for copy in own + small + [load]:
         copy.start()
 
     barrier = pltpu.get_barrier_semaphore()
@@ -156,18 +161,31 @@
 
         lax.fori_loop(0, 4, one, 0)
 
-    def mirror_slot(slot):
-        for k in range(2):
-            for h in range(2):
-                cols = slice(h * 512, h * 512 + 512)
-                wt[cols, k * 128:k * 128 + 128] = awi[2 + k, slot, :, cols].T
+    def mirror_slots(places, last=False):
+        slots = [slot_of(*place) for place in places]
+        for p, slot in enumerate(slots):
+            for k in range(2):
+                for h in range(2):
+                    cols = slice(h * 512, h * 512 + 512)
+                    start = (2 * p + k) * 128
+                    wt[cols, start:start + 128] = awi[2 + k, slot, :, cols].T
 
         def one(n, _):
             cols = pl.ds(pl.multiple_of(n * 256, 256), 256)
-            out[:, cols] += jnp.dot(wt[...], rmt[slot, :, cols], preferred_element_type=F32)
+            total = out[:, cols]
+            for p, slot in enumerate(slots):
+                total += jnp.dot(wt[:, p * 256:p * 256 + 256], rmt[slot, :, cols], preferred_element_type=F32)
+            out[:, cols] = amp[:, cols] + total * inv[:, cols] if last else total
             return _
 
         lax.fori_loop(0, 4, one, 0)
+
+    def inverse_rows(blk):
+        pair = el[0] + er[0]
+        turned = jnp.broadcast_to(ev[pl.ds(blk, 1), :], (128, 128)).T
+        for q in range(8):
+            virt_pair = turned + ev[q:q + 1, :]
+            inv[pl.ds(pl.multiple_of(blk * 128, 128), 128), q * 128:q * 128 + 128] = 1.0 / (pair - virt_pair)
 
     def loop(count, task):
         def one(n, _):
@@ -184,121 +202,129 @@
     ring_send("y", A1, True)
     x_send(0)
     send("zA0", i(A0, 0), "zi")
-    send("zA1", i(A1, 0), "zi")
     ring_send("y", W1, True)
-    send("zW0", i(W0, 0), "zi")
-    send("zW1.0", i(W1, 0), "zi")
+    for copy in small:
+        copy.wait()
+    loop(2, inverse_rows)
 
     x_forward(0)
+    ring_got("y", A0, True, "+")
+    ring_forward("y", A0, True, "+")
     got("jz+", j(0, -1))
     got("jz-", j(0, 1))
     send("jzf+", j(0, -1, 0, 2), "z+")
     send("jzf-", j(0, 1, 2, 4), "z-")
     x_send(-1)
     x_send(1)
-    ring_got("y", A0, True, "+")
-    ring_forward("y", A0, True, "+")
+    send("zA1", i(A1, 0), "zi")
+    send("zW0", i(W0, 0), "zi")
+    send("zW1.0", i(W1, 0), "zi")
     ring_got("y", A1, True, "-")
     ring_forward("y", A1, True, "-")
+    loop(2, lambda n: inverse_rows(n + 2))
     got("zA0", i(A0, 0, False))
     ring_send("p", A0, False)
-    got("zA1", i(A1, 0, False))
-    ring_send("p", A1, False)
-    got("jzf+", j(0, 2, 0, 2))
-    got("jzf-", j(0, 2, 2, 4))
-    x_send(2)
-    share(0)
-    x_got_forward(0)
-    x_forward(-1)
-    x_forward(1)
     ring_got("y", W1, True, "+")
     ring_got("y", W1, True, "-")
     send("zW1.-", i(W1, -1), "zi")
     send("zW1.+", i(W1, 1), "zi")
+    ring_forward("y", W1, True, "+", 0, 64)
+    ring_forward("y", W1, True, "-", 64, 128)
+    loop(2, lambda n: inverse_rows(n + 4))
+    got("jzf+", j(0, 2, 0, 2))
+    got("jzf-", j(0, 2, 2, 4))
+    x_send(2)
+    x_forward(-1)
+    x_forward(1)
+    x_got_forward(0)
+    share(0)
+    loop(2, lambda n: inverse_rows(n + 6))
+    got("zA1", i(A1, 0, False))
+    ring_send("p", A1, False)
+    ring_got("p", A0, False, "+")
+    ring_forward("p", A0, False, "+")
+    x_forward(2)
+    ring_got_forward("y", W1, True, "+", 0, 64)
+    ring_got_forward("y", W1, True, "-", 64, 128)
+    send("zW1.2", i(W1, 2), "zi")
+    ring_got("p", A1, False, "-")
+    ring_forward("p", A1, False, "-")
+    ring_send("y", W0, True)
+    got("zW0", i(W0, 0, False))
+    ring_send("p", W0, False)
+    x_got_forward(-1)
+    x_got_forward(1)
+    for dx in (-1, 1):
+        share(dx)
+    x_got_forward(2)
+    share(2)
+    for dx in (0, -1, 1, 2):
+        got_share(dx)
+    loop(8, mix_right)
     ring_got("y", A0, True, "-")
     ring_got("y", A1, True, "+")
     ring_got_forward("y", A0, True, "+")
     ring_got_forward("y", A1, True, "-")
-    ring_got("p", A0, False, "+")
-    ring_forward("p", A0, False, "+")
-    ring_got("p", A1, False, "-")
-    ring_forward("p", A1, False, "-")
-    ring_forward("y", W1, True, "+", 0, 64)
-    ring_forward("y", W1, True, "-", 64, 128)
-    ring_send("y", W0, True)
-    got("zW0", i(W0, 0, False))
-    ring_send("p", W0, False)
-    x_forward(2)
-    x_got_forward(-1)
-    x_got_forward(1)
-    x_got_forward(2)
-    for dx in (-1, 1, 2):
-        share(dx)
-    ring_got_forward("y", W1, True, "+", 0, 64)
-    ring_got_forward("y", W1, True, "-", 64, 128)
-    send("zW1.2", i(W1, 2), "zi")
     ring_got("p", A0, False, "-")
     ring_got("p", A1, False, "+")
     ring_got_forward("p", A0, False, "+")
     ring_got_forward("p", A1, False, "-")
     loop(8, mix_left)
-    for dx in (0, -1, 1, 2):
-        got_share(dx)
-    loop(8, mix_right)
+    direct_tile(0)
     ring_got("y", W0, True, "+")
     ring_got("y", W0, True, "-")
     ring_forward("y", W0, True, "+", 0, 64)
     ring_forward("y", W0, True, "-", 64, 128)
-    loop(4, direct_tile)
-    mirror_slot(slot_of(0, True))
+    loop(3, lambda n: direct_tile(n + 1))
     ring_got("p", W0, False, "+")
     ring_got("p", W0, False, "-")
     ring_forward("p", W0, False, "+", 0, 64)
     ring_forward("p", W0, False, "-", 64, 128)
-    mirror_slot(slot_of(-1, True))
-    mirror_slot(slot_of(1, True))
     got("zW1.0", i(W1, 0, False))
-    mirror_slot(slot_of(0, False))
+    mirror_slots([(0, True), (0, False)])
+    mirror_slots([(-1, True), (1, True)])
     got("zW1.-", i(W1, -1, False))
-    mirror_slot(slot_of(-1, False))
     got("zW1.+", i(W1, 1, False))
-    mirror_slot(slot_of(1, False))
+    mirror_slots([(-1, False), (1, False)])
+    load.wait()
     ring_got_forward("y", W0, True, "+", 0, 64)
     ring_got_forward("y", W0, True, "-", 64, 128)
-    mirror_slot(slot_of(2, True))
     got("zW1.2", i(W1, 2, False))
     ring_got_forward("p", W0, False, "+", 0, 64)
     ring_got_forward("p", W0, False, "-", 64, 128)
-    mirror_slot(slot_of(2, False))
+    mirror_slots([(2, True), (2, False)], True)
     for copy in sent:
         copy.wait_send()
     assert len(ids) <= N_MSG
 
 
 def body(amplitudes, panels_left, panels_right, weights_right, weights_left, energy_left, energy_right, energy_virtual):
-    residual = pl.pallas_call(
+    updated = pl.pallas_call(
         gather_kernel,
         out_shape=jax.ShapeDtypeStruct((1024, 1024), F32),
-        in_specs=[pl.BlockSpec(memory_space=pl.ANY)] * 4,
+        in_specs=[pl.BlockSpec(memory_space=pltpu.HBM)] * 6 + [pl.BlockSpec(memory_space=pltpu.SMEM)] * 2,
         out_specs=pl.BlockSpec(memory_space=pltpu.VMEM),
         scratch_shapes=[
             pltpu.VMEM((4, 8, 128, 1024), BF16),
             pltpu.VMEM((4, 4, 4, 2, 32, 1024), BF16),
             pltpu.VMEM((2, 1024, 1024), BF16),
             pltpu.VMEM((8, 256, 1024), BF16),
-            pltpu.VMEM((1024, 256), BF16),
-            pltpu.SemaphoreType.DMA((4,)),
+            pltpu.VMEM((1024, 512), BF16),
+            pltpu.VMEM((1024, 1024), F32),
+            pltpu.VMEM((1024, 1024), F32),
+            pltpu.VMEM((8, 128), F32),
+            pltpu.SemaphoreType.DMA((6,)),
             pltpu.SemaphoreType.DMA((N_MSG,)),
             pltpu.SemaphoreType.DMA((N_MSG,)),
         ],
         compiler_params=pltpu.CompilerParams(
-            collective_id=0, has_side_effects=True, vmem_limit_bytes=44 * 1024 * 1024
+            collective_id=0, has_side_effects=True, vmem_limit_bytes=48 * 1024 * 1024
         ),
         name="gather_products",
-    )(panels_left[0], panels_right[0], weights_right[:, 0], weights_left[:, 0])
-    virt_pair = energy_virtual[:, None] + energy_virtual[None, :]
-    denominator = energy_left[0] + energy_right[0] - virt_pair
-    return (amplitudes[0, 0] + residual / denominator)[None, None]
+    )(*(pltpu.with_memory_space_constraint(array, pltpu.HBM) for array in (
+        panels_left[0], panels_right[0], weights_right[:, 0], weights_left[:, 0], amplitudes[0, 0],
+        energy_virtual.reshape(8, 128))), energy_left, energy_right)
+    return updated[None, None]
 
 
 def solution(mesh):

time: 104 us -> 80.2 us (0.77)
  Pallas kernels: 95.6 us -> 76.8 us
  other arithmetic: 2.77 us -> 0 us
  local copies, waits for them, and re-layouts: 3.89 us -> 2.02 us
    pallas_call x1, Pallas kernels: 95.6 us -> 76.8 us  [body(): pl.pallas_call(gather_kernel, out_shape=jax.ShapeDtypeStruct((1024, 1024)...]
    broadcast_in_dim x1 -> x0, other arithmetic: 2.77 us -> none  [body(): return (amplitudes[0, 0] + residual / denominator)[None, None]]
    unnamed x12 -> x1, local copies, waits for them, and re-layouts: 3.89 us -> 2.02 us
where the time goes in v2:
time: 80.2 us; the launch traced here: 80.1 us
  Pallas kernels  76.8 us (96%)
  local copies, waits for them, and re-layouts  2.02 us (3%)
  between operations  1.3 us (2%)
    pallas_call x1, Pallas kernels, body(): pl.pallas_call(gather_kernel, out_shape=jax.ShapeDtypeStruct((1024, 1024)...  76.8 us
    unnamed x1, local copies, waits for them, and re-layouts  2.02 us

profile of v2, /device:TPU:1, one launch (start us, length us, event | category | flops | bytes accessed | tf_op | source)
XLA Modules:
  0.0 80.1 jit_solution(8524064996348647990)
XLA Ops:
  1.3 76.8 %gather_products.1 = f32[1024,1024]{1,0:T(8,128)S(1)} custom-call(bf16[2,128,1024]{2,1,0:T(8,128)(2,1)} %bitcast.9, bf16[2,32,1024]{2,1,0:T(8,128)(2,1)} %bitcast.11, bf16[2,32,1024]{2,1,0:T(8,128)(2,1)} %bitcast.12, bf16[2,128,1024]{2,1,0:T(8,128)(2,1)} %bitcast.10, f32[1024,1024]{1,0:T(8,128)} %bitcast.8, f32[8,128]{1,0:T(8,128)} %bitcast.13, ...), custom_call_target="tpu_custom_call" | custom-call | tf_op jit(solution)/shard_map/gather_products/pallas_call | solution.py:302
  78.1 2.0 %copy.12 = f32[1,1,1024,1024]{3,2,1,0:T(8,128)} copy(f32[1,1,1024,1024]{3,2,1,0:T(8,128)S(1)} %bitcast.7) | data formatting | bytes 8388608

commit v3 on v2

--- a/solution.py
+++ b/solution.py
@@ -9,9 +9,10 @@
 F32 = jnp.float32
 BF16 = jnp.bfloat16
 N_MSG = 56
-
-
-def gather_kernel(panl, panr, wtr, wtl, amp_in, ev_in, el, er, out, awi, awj, lm, rmt, wt, amp, inv, ev,
+CUT = 112
+
+
+def gather_kernel(panl, panr, wtr, wtl, amp_in, ev_in, el, er, out, inv, wt, rmt, awi, awj, lm, amp, ev,
                   lsem, ssem, rsem):
     row, col = lax.axis_index("row"), lax.axis_index("col")
     x, zh, core = row // 8, lax.rem(row // 2, 4), lax.rem(row, 2)
@@ -41,10 +42,10 @@
     }
 
     own = [
-        pltpu.make_async_copy(panl, awi.at[0:2, col], lsem.at[0]),
+        pltpu.make_async_copy(panl, awi.at[col, 0:256], lsem.at[0]),
         pltpu.make_async_copy(panr, awj.at[0:2, x, zh, core], lsem.at[1]),
         pltpu.make_async_copy(wtr, awj.at[2:4, x, zh, core], lsem.at[2]),
-        pltpu.make_async_copy(wtl, awi.at[2:4, col], lsem.at[3]),
+        pltpu.make_async_copy(wtl, awi.at[col, 256:512], lsem.at[3]),
     ]
     small = [
         pltpu.make_async_copy(ev_in, ev, lsem.at[4]),
@@ -81,25 +82,26 @@
     def j(dx, dz, lo=0, hi=4):
         return awj.at[lo:hi, at_x(dx), at_z(dz), core]
 
-    def i(part, dy, same=True, lo=0, hi=128):
-        return awi.at[part, (zl if same else 1 - zl) * 4 + at_y(dy), lo:hi]
-
-    A0, A1, W0, W1 = 0, 1, 2, 3
-    OPP = {"+": "-", "-": "+"}
+    def i(part, dy, same=True):
+        return awi.at[(zl if same else 1 - zl) * 4 + at_y(dy), part[0]:part[1]]
+
+    A0, A1, U, V = (0, 128), (128, 256), (256, 256 + CUT), (256 + CUT, 512)
+    UP = {"+": (256, 320), "-": (320, 256 + CUT)}
+    VP = {"+": (256 + CUT, 320 + CUT), "-": (320 + CUT, 512)}
     STEP = {"+": 1, "-": -1}
 
-    def ring_send(tag, part, same, signs="+-"):
-        for s in signs:
+    def ring_send(tag, part, same):
+        for s in "+-":
             send(f"{tag}{part}{s}", i(part, 0, same), "y" + s)
 
     def ring_got(tag, part, same, s):
         got(f"{tag}{part}{s}", i(part, -STEP[s], same))
 
-    def ring_forward(tag, part, same, s, lo=0, hi=128):
-        send(f"{tag}f{part}{s}", i(part, -STEP[s], same, lo, hi), "y" + s)
-
-    def ring_got_forward(tag, part, same, s, lo=0, hi=128):
-        got(f"{tag}f{part}{s}", i(part, 2, same, lo, hi))
+    def ring_forward(tag, part, same, s):
+        send(f"{tag}f{part}{s}", i(part, -STEP[s], same), "y" + s)
+
+    def ring_got_forward(tag, part, same, s):
+        got(f"{tag}f{part}{s}", i(part, 2, same))
 
     def x_send(dz):
         for s in "+-":
@@ -125,10 +127,11 @@
         start = pl.multiple_of(blk * 128, 128)
 
         def one(k, _):
+            own_rows = pl.ds(pl.multiple_of(k * 128, 128), 128)
             for h in range(2):
                 cols = slice(h * 512, h * 512 + 512)
-                straight = awi[k, blk, :, cols].astype(F32)
-                turned = awi[k, h * 4:h * 4 + 4, :, pl.ds(start, 128)].reshape(512, 128).T.astype(F32)
+                straight = awi[blk, own_rows, cols].astype(F32)
+                turned = awi[h * 4:h * 4 + 4, own_rows, pl.ds(start, 128)].reshape(512, 128).T.astype(F32)
                 lm[k, pl.ds(start, 128), cols] = (2.0 * straight - turned).astype(BF16)
             return _
 
@@ -147,38 +150,33 @@
 
         lax.fori_loop(0, 2, one, 0)
 
-    def direct_tile(m):
-        rows = pl.ds(pl.multiple_of(m * 256, 256), 256)
-
-        def one(n, _):
-            cols = pl.ds(pl.multiple_of(n * 256, 256), 256)
-            total = jnp.zeros((256, 256), F32)
-            for k in range(2):
-                total += jnp.dot(lm[k, rows, :], awj[2 + k, :, :, :, :, cols].reshape(1024, 256),
-                                 preferred_element_type=F32)
-            out[rows, cols] = total
-            return _
-
-        lax.fori_loop(0, 4, one, 0)
-
-    def mirror_slots(places, last=False):
+    def direct_tile(n):
+        cols = pl.ds(pl.multiple_of(n * 512, 512), 512)
+        total = jnp.dot(lm[0], awj[2, :, :, :, :, cols].reshape(1024, 512), preferred_element_type=F32)
+        total += jnp.dot(lm[1], awj[3, :, :, :, :, cols].reshape(1024, 512), preferred_element_type=F32)
+        out[:, cols] += total
+
+    def turn(p, slot):
+        for k in range(2):
+            for h in range(2):
+                cols = slice(h * 512, h * 512 + 512)
+                start = (2 * p + k) * 128
+                wt[cols, start:start + 128] = awi[slot, 256 + k * 128:384 + k * 128, cols].T
+
+    def mirror_slots(places, first=False, last=False):
         slots = [slot_of(*place) for place in places]
         for p, slot in enumerate(slots):
-            for k in range(2):
-                for h in range(2):
-                    cols = slice(h * 512, h * 512 + 512)
-                    start = (2 * p + k) * 128
-                    wt[cols, start:start + 128] = awi[2 + k, slot, :, cols].T
+            turn(p, slot)
 
         def one(n, _):
-            cols = pl.ds(pl.multiple_of(n * 256, 256), 256)
-            total = out[:, cols]
+            cols = pl.ds(pl.multiple_of(n * 512, 512), 512)
+            total = jnp.zeros((1024, 512), F32) if first else out[:, cols]
             for p, slot in enumerate(slots):
                 total += jnp.dot(wt[:, p * 256:p * 256 + 256], rmt[slot, :, cols], preferred_element_type=F32)
             out[:, cols] = amp[:, cols] + total * inv[:, cols] if last else total
             return _
 
-        lax.fori_loop(0, 4, one, 0)
+        lax.fori_loop(0, 2, one, 0)
 
     def inverse_rows(blk):
         pair = el[0] + er[0]
@@ -202,7 +200,7 @@
     ring_send("y", A1, True)
     x_send(0)
     send("zA0", i(A0, 0), "zi")
-    ring_send("y", W1, True)
+    ring_send("y", V, True)
     for copy in small:
         copy.wait()
     loop(2, inverse_rows)
@@ -217,19 +215,19 @@
     x_send(-1)
     x_send(1)
     send("zA1", i(A1, 0), "zi")
-    send("zW0", i(W0, 0), "zi")
-    send("zW1.0", i(W1, 0), "zi")
+    send("zU", i(U, 0), "zi")
+    send("zV.0", i(V, 0), "zi")
     ring_got("y", A1, True, "-")
     ring_forward("y", A1, True, "-")
     loop(2, lambda n: inverse_rows(n + 2))
     got("zA0", i(A0, 0, False))
     ring_send("p", A0, False)
-    ring_got("y", W1, True, "+")
-    ring_got("y", W1, True, "-")
-    send("zW1.-", i(W1, -1), "zi")
-    send("zW1.+", i(W1, 1), "zi")
-    ring_forward("y", W1, True, "+", 0, 64)
-    ring_forward("y", W1, True, "-", 64, 128)
+    ring_got("y", V, True, "+")
+    ring_got("y", V, True, "-")
+    send("zV.-", i(V, -1), "zi")
+    send("zV.+", i(V, 1), "zi")
+    ring_forward("y", VP["+"], True, "+")
+    ring_forward("y", VP["-"], True, "-")
     loop(2, lambda n: inverse_rows(n + 4))
     got("jzf+", j(0, 2, 0, 2))
     got("jzf-", j(0, 2, 2, 4))
@@ -244,14 +242,14 @@
     ring_got("p", A0, False, "+")
     ring_forward("p", A0, False, "+")
     x_forward(2)
-    ring_got_forward("y", W1, True, "+", 0, 64)
-    ring_got_forward("y", W1, True, "-", 64, 128)
-    send("zW1.2", i(W1, 2), "zi")
+    ring_got_forward("y", VP["+"], True, "+")
+    ring_got_forward("y", VP["-"], True, "-")
+    send("zV.2", i(V, 2), "zi")
     ring_got("p", A1, False, "-")
     ring_forward("p", A1, False, "-")
-    ring_send("y", W0, True)
-    got("zW0", i(W0, 0, False))
-    ring_send("p", W0, False)
+    ring_send("y", U, True)
+    got("zU", i(U, 0, False))
+    ring_send("p", U, False)
     x_got_forward(-1)
     x_got_forward(1)
     for dx in (-1, 1):
@@ -261,6 +259,7 @@
     for dx in (0, -1, 1, 2):
         got_share(dx)
     loop(8, mix_right)
+    mirror_slots([(0, True)], first=True)
     ring_got("y", A0, True, "-")
     ring_got("y", A1, True, "+")
     ring_got_forward("y", A0, True, "+")
@@ -271,46 +270,63 @@
     ring_got_forward("p", A1, False, "-")
     loop(8, mix_left)
     direct_tile(0)
-    ring_got("y", W0, True, "+")
-    ring_got("y", W0, True, "-")
-    ring_forward("y", W0, True, "+", 0, 64)
-    ring_forward("y", W0, True, "-", 64, 128)
-    loop(3, lambda n: direct_tile(n + 1))
-    ring_got("p", W0, False, "+")
-    ring_got("p", W0, False, "-")
-    ring_forward("p", W0, False, "+", 0, 64)
-    ring_forward("p", W0, False, "-", 64, 128)
-    got("zW1.0", i(W1, 0, False))
-    mirror_slots([(0, True), (0, False)])
-    mirror_slots([(-1, True), (1, True)])
-    got("zW1.-", i(W1, -1, False))
-    got("zW1.+", i(W1, 1, False))
-    mirror_slots([(-1, False), (1, False)])
+    ring_got("y", U, True, "+")
+    ring_forward("y", UP["+"], True, "+")
+    ring_got("y", U, True, "-")
+    ring_forward("y", UP["-"], True, "-")
+    direct_tile(1)
+    ring_got("p", U, False, "+")
+    ring_forward("p", UP["+"], False, "+")
+    ring_got("p", U, False, "-")
+    ring_forward("p", UP["-"], False, "-")
+    got("zV.0", i(V, 0, False))
+    mirror_slots([(-1, True), (1, True), (0, False)])
+    got("zV.-", i(V, -1, False))
+    got("zV.+", i(V, 1, False))
     load.wait()
-    ring_got_forward("y", W0, True, "+", 0, 64)
-    ring_got_forward("y", W0, True, "-", 64, 128)
-    got("zW1.2", i(W1, 2, False))
-    ring_got_forward("p", W0, False, "+", 0, 64)
-    ring_got_forward("p", W0, False, "-", 64, 128)
-    mirror_slots([(2, True), (2, False)], True)
-    for copy in sent:
+    ring_got_forward("y", UP["+"], True, "+")
+    ring_got_forward("y", UP["-"], True, "-")
+    mirror_slots([(-1, False), (1, False), (2, True)], last=True)
+    for copy in sent[:-6]:
+        copy.wait_send()
+    got("zV.2", i(V, 2, False))
+    ring_got_forward("p", UP["+"], False, "+")
+    ring_got_forward("p", UP["-"], False, "-")
+    turn(0, slot_of(2, False))
+    for copy in sent[-6:]:
         copy.wait_send()
     assert len(ids) <= N_MSG
 
 
+def finish_kernel(base, inv, wt, rmt, result, stage, sem):
+    col = lax.axis_index("col")
+    slot = (1 - col // 4) * 4 + lax.rem(col + 2, 4)
+    copies = []
+    for m in range(4):
+        rows = slice(m * 256, m * 256 + 256)
+        total = jnp.dot(wt[rows, :256], rmt[slot], preferred_element_type=F32)
+        stage[rows] = base[rows] + total * inv[rows]
+        copies.append(pltpu.make_async_copy(stage.at[rows], result.at[rows], sem.at[m]))
+        copies[-1].start()
+    for copy in copies:
+        copy.wait()
+
+
 def body(amplitudes, panels_left, panels_right, weights_right, weights_left, energy_left, energy_right, energy_virtual):
-    updated = pl.pallas_call(
+    middle = pl.pallas_call(
         gather_kernel,
-        out_shape=jax.ShapeDtypeStruct((1024, 1024), F32),
+        out_shape=[
+            jax.ShapeDtypeStruct((1024, 1024), F32),
+            jax.ShapeDtypeStruct((1024, 1024), F32),
+            jax.ShapeDtypeStruct((1024, 768), BF16),
+            jax.ShapeDtypeStruct((8, 256, 1024), BF16),
+        ],
         in_specs=[pl.BlockSpec(memory_space=pltpu.HBM)] * 6 + [pl.BlockSpec(memory_space=pltpu.SMEM)] * 2,
-        out_specs=pl.BlockSpec(memory_space=pltpu.VMEM),
+        out_specs=[pl.BlockSpec(memory_space=pltpu.VMEM)] * 4,
         scratch_shapes=[
-            pltpu.VMEM((4, 8, 128, 1024), BF16),
+            pltpu.VMEM((8, 512, 1024), BF16),
             pltpu.VMEM((4, 4, 4, 2, 32, 1024), BF16),
             pltpu.VMEM((2, 1024, 1024), BF16),
-            pltpu.VMEM((8, 256, 1024), BF16),
-            pltpu.VMEM((1024, 512), BF16),
-            pltpu.VMEM((1024, 1024), F32),
             pltpu.VMEM((1024, 1024), F32),
             pltpu.VMEM((8, 128), F32),
             pltpu.SemaphoreType.DMA((6,)),
@@ -318,12 +334,22 @@
             pltpu.SemaphoreType.DMA((N_MSG,)),
         ],
         compiler_params=pltpu.CompilerParams(
-            collective_id=0, has_side_effects=True, vmem_limit_bytes=48 * 1024 * 1024
+            collective_id=0, has_side_effects=True, vmem_limit_bytes=36 * 1024 * 1024
         ),
         name="gather_products",
     )(*(pltpu.with_memory_space_constraint(array, pltpu.HBM) for array in (
-        panels_left[0], panels_right[0], weights_right[:, 0], weights_left[:, 0], amplitudes[0, 0],
+        panels_left.reshape(256, 1024), panels_right[0], weights_right[:, 0], weights_left.reshape(256, 1024),
+        amplitudes[0, 0],
         energy_virtual.reshape(8, 128))), energy_left, energy_right)
+    updated = pl.pallas_call(
+        finish_kernel,
+        out_shape=jax.ShapeDtypeStruct((1024, 1024), F32),
+        in_specs=[pl.BlockSpec(memory_space=pltpu.VMEM)] * 4,
+        out_specs=pl.BlockSpec(memory_space=pltpu.HBM),
+        scratch_shapes=[pltpu.VMEM((1024, 1024), F32), pltpu.SemaphoreType.DMA((4,))],
+        compiler_params=pltpu.CompilerParams(vmem_limit_bytes=12 * 1024 * 1024),
+        name="finish",
+    )(*middle)
     return updated[None, None]
 
 

time: 80.2 us -> 75.5 us (0.941)
  Pallas kernels: 76.8 us -> 74.1 us
  local copies, waits for them, and re-layouts: 2.02 us -> 0 us
    pallas_call x1 -> x2, Pallas kernels: 76.8 us -> 74.1 us  [the longest x1 71.7 us: body(): pl.pallas_call(gather_kernel, out_shape=[jax.ShapeDtypeStruct((1024, 1024...]
    unnamed x1 -> x0, local copies, waits for them, and re-layouts: 2.02 us -> none
where the time goes in v3:
time: 75.5 us; the launch traced here: 75.4 us
  Pallas kernels  74.1 us (98%)
  between operations  1.3 us (2%)
    pallas_call x1, Pallas kernels, body(): pl.pallas_call(gather_kernel, out_shape=[jax.ShapeDtypeStruct((1024, 1024...  71.7 us
    pallas_call x1, Pallas kernels, body(): pl.pallas_call(finish_kernel, out_shape=jax.ShapeDtypeStruct((1024, 1024)...  2.36 us

profile of v3, /device:TPU:1, one launch (start us, length us, event | category | flops | bytes accessed | tf_op | source)
XLA Modules:
  0.0 75.4 jit_solution(737167426388939243)
XLA Ops:
  1.3 71.7 %gather_products.1 = (f32[1024,1024]{1,0:T(8,128)S(1)}, f32[1024,1024]{1,0:T(8,128)S(1)}, bf16[1024,768]{1,0:T(8,128)(2,1)S(1)}, bf16[8,256,1024]{2,1,0:T(8,128)(2,1)S(1)}) custom-call(bf16[256,1024]{1,0:T(8,128)(2,1)} %bitcast.8, bf16[2,32,1024]{2,1,0:T(8,128)(2,1)} %bitcast.10, bf16[2,32,1024]{2,1,0:T(8,128)(2,1)} %bitcast.11, bf16[256,1024]{1,0:T(8,128)(2,1)} %bitcast.9, ...), custom_call_target="tpu_custom_call" | custom-call | tf_op jit(solution)/shard_map/gather_products/pallas_call | solution.py:316
  73.0 2.4 %finish.1 = f32[1024,1024]{1,0:T(8,128)} custom-call(f32[1024,1024]{1,0:T(8,128)S(1)} %get-tuple-element.9.base, f32[1024,1024]{1,0:T(8,128)S(1)} %get-tuple-element.10.inv, bf16[1024,768]{1,0:T(8,128)(2,1)S(1)} %get-tuple-element.11.wt, bf16[8,256,1024]{2,1,0:T(8,128)(2,1)S(1)} %get-tuple-element.12.rmt), custom_call_target="tpu_custom_call" | custom-call | tf_op jit(solution)/shard_map/finish/pallas_call | solution.py:344

commit v4 on v3

--- a/solution.py
+++ b/solution.py
@@ -9,6 +9,7 @@
 F32 = jnp.float32
 BF16 = jnp.bfloat16
 N_MSG = 56
+BLOCKS = ((0, 256), (256, 256), (512, 256), (768, 256))
 CUT = 112
 
 
@@ -51,15 +52,13 @@
         pltpu.make_async_copy(ev_in, ev, lsem.at[4]),
     ]
     load = pltpu.make_async_copy(amp_in, amp, lsem.at[5])
-    for copy in own + small + [load]:
+    for copy in (own[1], own[2], own[0], own[3], *small):
         copy.start()
 
     barrier = pltpu.get_barrier_semaphore()
     for peer in dev.values():
         pl.semaphore_signal(barrier, inc=1, device_id=peer, device_id_type=MESH)
     pl.semaphore_wait(barrier, len(dev))
-    for copy in own:
-        copy.wait()
 
     ids = {}
     sent = []
@@ -87,7 +86,7 @@
 
     A0, A1, U, V = (0, 128), (128, 256), (256, 256 + CUT), (256 + CUT, 512)
     UP = {"+": (256, 320), "-": (320, 256 + CUT)}
-    VP = {"+": (256 + CUT, 320 + CUT), "-": (320 + CUT, 512)}
+    VP = {"+": (256 + CUT, 320 + CUT), "-": (320 + CUT, 464), "late": (464, 512)}
     STEP = {"+": 1, "-": -1}
 
     def ring_send(tag, part, same):
@@ -123,19 +122,14 @@
     def got_share(dx):
         got(f"core{dx}", awj.at[:, at_x(dx), :, 1 - core])
 
-    def mix_left(blk):
+    def mix_left(k, blk):
         start = pl.multiple_of(blk * 128, 128)
-
-        def one(k, _):
-            own_rows = pl.ds(pl.multiple_of(k * 128, 128), 128)
-            for h in range(2):
-                cols = slice(h * 512, h * 512 + 512)
-                straight = awi[blk, own_rows, cols].astype(F32)
-                turned = awi[h * 4:h * 4 + 4, own_rows, pl.ds(start, 128)].reshape(512, 128).T.astype(F32)
-                lm[k, pl.ds(start, 128), cols] = (2.0 * straight - turned).astype(BF16)
-            return _
-
-        lax.fori_loop(0, 2, one, 0)
+        own_rows = slice(k * 128, k * 128 + 128)
+        for h in range(2):
+            cols = slice(h * 512, h * 512 + 512)
+            straight = awi[blk, own_rows, cols]
+            turned = awi[h * 4:h * 4 + 4, own_rows, pl.ds(start, 128)].reshape(512, 128).T
+            lm[k, pl.ds(start, 128), cols] = straight + straight - turned
 
     def mix_right(blk):
         start = pl.multiple_of(blk * 128, 128)
@@ -143,9 +137,9 @@
         def one(k, _):
             for h in range(2):
                 cols = slice(h * 512, h * 512 + 512)
-                straight = awj[k, blk // 2, pl.ds(lax.rem(blk, 2) * 2, 2), :, :, cols].reshape(128, 512).astype(F32)
-                turned = awj[k, h * 2:h * 2 + 2, :, :, :, pl.ds(start, 128)].reshape(512, 128).T.astype(F32)
-                rmt[blk, pl.ds(pl.multiple_of(k * 128, 128), 128), cols] = (2.0 * turned - straight).astype(BF16)
+                straight = awj[k, blk // 2, pl.ds(lax.rem(blk, 2) * 2, 2), :, :, cols].reshape(128, 512)
+                turned = awj[k, h * 2:h * 2 + 2, :, :, :, pl.ds(start, 128)].reshape(512, 128).T
+                rmt[blk, pl.ds(pl.multiple_of(k * 128, 128), 128), cols] = turned + turned - straight
             return _
 
         lax.fori_loop(0, 2, one, 0)
@@ -194,13 +188,18 @@
     def slot_of(dy, same):
         return (zl if same else 1 - zl) * 4 + at_y(dy)
 
+    own[1].wait()
+    own[2].wait()
     send("jz+", j(0, 0), "z+")
     send("jz-", j(0, 0), "z-")
+    own[0].wait()
     ring_send("y", A0, True)
     ring_send("y", A1, True)
     x_send(0)
     send("zA0", i(A0, 0), "zi")
+    own[3].wait()
     ring_send("y", V, True)
+    load.start()
     for copy in small:
         copy.wait()
     loop(2, inverse_rows)
@@ -239,15 +238,17 @@
     loop(2, lambda n: inverse_rows(n + 6))
     got("zA1", i(A1, 0, False))
     ring_send("p", A1, False)
+    ring_forward("y", VP["late"], True, "-")
     ring_got("p", A0, False, "+")
     ring_forward("p", A0, False, "+")
     x_forward(2)
-    ring_got_forward("y", VP["+"], True, "+")
-    ring_got_forward("y", VP["-"], True, "-")
-    send("zV.2", i(V, 2), "zi")
     ring_got("p", A1, False, "-")
     ring_forward("p", A1, False, "-")
     ring_send("y", U, True)
+    ring_got_forward("y", VP["+"], True, "+")
+    ring_got_forward("y", VP["-"], True, "-")
+    ring_got_forward("y", VP["late"], True, "-")
+    send("zV.2", i(V, 2), "zi")
     got("zU", i(U, 0, False))
     ring_send("p", U, False)
     x_got_forward(-1)
@@ -261,14 +262,15 @@
     loop(8, mix_right)
     mirror_slots([(0, True)], first=True)
     ring_got("y", A0, True, "-")
+    ring_got_forward("y", A0, True, "+")
+    ring_got("p", A0, False, "-")
+    ring_got_forward("p", A0, False, "+")
+    loop(8, lambda n: mix_left(0, n))
     ring_got("y", A1, True, "+")
-    ring_got_forward("y", A0, True, "+")
     ring_got_forward("y", A1, True, "-")
-    ring_got("p", A0, False, "-")
     ring_got("p", A1, False, "+")
-    ring_got_forward("p", A0, False, "+")
     ring_got_forward("p", A1, False, "-")
-    loop(8, mix_left)
+    loop(8, lambda n: mix_left(1, n))
     direct_tile(0)
     ring_got("y", U, True, "+")
     ring_forward("y", UP["+"], True, "+")
@@ -302,8 +304,8 @@
     col = lax.axis_index("col")
     slot = (1 - col // 4) * 4 + lax.rem(col + 2, 4)
     copies = []
-    for m in range(4):
-        rows = slice(m * 256, m * 256 + 256)
+    for m, (start, size) in enumerate(BLOCKS):
+        rows = slice(start, start + size)
         total = jnp.dot(wt[rows, :256], rmt[slot], preferred_element_type=F32)
         stage[rows] = base[rows] + total * inv[rows]
         copies.append(pltpu.make_async_copy(stage.at[rows], result.at[rows], sem.at[m]))
@@ -346,7 +348,7 @@
         out_shape=jax.ShapeDtypeStruct((1024, 1024), F32),
         in_specs=[pl.BlockSpec(memory_space=pltpu.VMEM)] * 4,
         out_specs=pl.BlockSpec(memory_space=pltpu.HBM),
-        scratch_shapes=[pltpu.VMEM((1024, 1024), F32), pltpu.SemaphoreType.DMA((4,))],
+        scratch_shapes=[pltpu.VMEM((1024, 1024), F32), pltpu.SemaphoreType.DMA((len(BLOCKS),))],
         compiler_params=pltpu.CompilerParams(vmem_limit_bytes=12 * 1024 * 1024),
         name="finish",
     )(*middle)

time: 75.5 us -> 74.8 us (level)
  no operation moved by 1% of the time
where the time goes in v4:
time: 74.8 us; the launch traced here: 74.7 us
  Pallas kernels  73.4 us (98%)
  between operations  1.3 us (2%)
    pallas_call x1, Pallas kernels, body(): pl.pallas_call(gather_kernel, out_shape=[jax.ShapeDtypeStruct((1024, 1024...  71 us
    pallas_call x1, Pallas kernels, body(): pl.pallas_call(finish_kernel, out_shape=jax.ShapeDtypeStruct((1024, 1024)...  2.36 us

profile of v4, /device:TPU:1, one launch (start us, length us, event | category | flops | bytes accessed | tf_op | source)
XLA Modules:
  0.0 74.7 jit_solution(155075674405872177)
XLA Ops:
  1.3 71.0 %gather_products.1 = (f32[1024,1024]{1,0:T(8,128)S(1)}, f32[1024,1024]{1,0:T(8,128)S(1)}, bf16[1024,768]{1,0:T(8,128)(2,1)S(1)}, bf16[8,256,1024]{2,1,0:T(8,128)(2,1)S(1)}) custom-call(bf16[256,1024]{1,0:T(8,128)(2,1)} %bitcast.8, bf16[2,32,1024]{2,1,0:T(8,128)(2,1)} %bitcast.10, bf16[2,32,1024]{2,1,0:T(8,128)(2,1)} %bitcast.11, bf16[256,1024]{1,0:T(8,128)(2,1)} %bitcast.9, ...), custom_call_target="tpu_custom_call" | custom-call | tf_op jit(solution)/shard_map/gather_products/pallas_call | solution.py:318
  72.3 2.4 %finish.1 = f32[1024,1024]{1,0:T(8,128)} custom-call(f32[1024,1024]{1,0:T(8,128)S(1)} %get-tuple-element.9.base, f32[1024,1024]{1,0:T(8,128)S(1)} %get-tuple-element.10.inv, bf16[1024,768]{1,0:T(8,128)(2,1)S(1)} %get-tuple-element.11.wt, bf16[8,256,1024]{2,1,0:T(8,128)(2,1)S(1)} %get-tuple-element.12.rmt), custom_call_target="tpu_custom_call" | custom-call | tf_op jit(solution)/shard_map/finish/pallas_call | solution.py:346

commit v5 on v4

--- a/solution.py
+++ b/solution.py
@@ -131,18 +131,15 @@
             turned = awi[h * 4:h * 4 + 4, own_rows, pl.ds(start, 128)].reshape(512, 128).T
             lm[k, pl.ds(start, 128), cols] = straight + straight - turned
 
-    def mix_right(blk):
-        start = pl.multiple_of(blk * 128, 128)
-
-        def one(k, _):
-            for h in range(2):
-                cols = slice(h * 512, h * 512 + 512)
-                straight = awj[k, blk // 2, pl.ds(lax.rem(blk, 2) * 2, 2), :, :, cols].reshape(128, 512)
-                turned = awj[k, h * 2:h * 2 + 2, :, :, :, pl.ds(start, 128)].reshape(512, 128).T
-                rmt[blk, pl.ds(pl.multiple_of(k * 128, 128), 128), cols] = turned + turned - straight
-            return _
-
-        lax.fori_loop(0, 2, one, 0)
+    def mix_right(d1, d2):
+        g1, g2 = at_x(d1), at_x(d2)
+        cols = pl.ds(pl.multiple_of(g2 * 256, 256), 256)
+        for k in range(2):
+            for half in range(2):
+                blk = g1 * 2 + half
+                turned = awj[k, g2, :, :, :, pl.ds(pl.multiple_of(blk * 128, 128), 128)].reshape(256, 128).T
+                straight = awj[k, g1, 2 * half:2 * half + 2, :, :, cols].reshape(128, 256)
+                rmt[blk, k * 128:k * 128 + 128, cols] = turned + turned - straight
 
     def direct_tile(n):
         cols = pl.ds(pl.multiple_of(n * 512, 512), 512)
@@ -251,15 +248,18 @@
     send("zV.2", i(V, 2), "zi")
     got("zU", i(U, 0, False))
     ring_send("p", U, False)
+    for dx in (-1, 1):
+        share(dx)
+    for dx in (0, -1, 1):
+        got_share(dx)
+    loop(9, lambda n: mix_right(n // 3 - 1, lax.rem(n, 3) - 1))
     x_got_forward(-1)
     x_got_forward(1)
-    for dx in (-1, 1):
-        share(dx)
     x_got_forward(2)
     share(2)
-    for dx in (0, -1, 1, 2):
-        got_share(dx)
-    loop(8, mix_right)
+    got_share(2)
+    loop(4, lambda n: mix_right(2, n - 1))
+    loop(3, lambda n: mix_right(n - 1, 2))
     mirror_slots([(0, True)], first=True)
     ring_got("y", A0, True, "-")
     ring_got_forward("y", A0, True, "+")

time: 74.8 us -> 74.5 us (level); the launches traced: 74.7 us -> 73.2 us
  Pallas kernels: 73.4 us -> 71.9 us
    pallas_call x1, Pallas kernels: 71 us -> 69.6 us  [body(): pl.pallas_call(gather_kernel, out_shape=[jax.ShapeDtypeStruct((1024, 1024...]
where the time goes in v5:
time: 74.5 us; the launch traced here: 73.2 us
  Pallas kernels  71.9 us (97%)
  between operations  1.3 us (2%)
    pallas_call x1, Pallas kernels, body(): pl.pallas_call(gather_kernel, out_shape=[jax.ShapeDtypeStruct((1024, 1024...  69.6 us
    pallas_call x1, Pallas kernels, body(): pl.pallas_call(finish_kernel, out_shape=jax.ShapeDtypeStruct((1024, 1024)...  2.36 us

profile of v5, /device:TPU:1, one launch (start us, length us, event | category | flops | bytes accessed | tf_op | source)
XLA Modules:
  0.0 73.2 jit_solution(2323387202565271138)
XLA Ops:
  1.3 69.6 %gather_products.1 = (f32[1024,1024]{1,0:T(8,128)S(1)}, f32[1024,1024]{1,0:T(8,128)S(1)}, bf16[1024,768]{1,0:T(8,128)(2,1)S(1)}, bf16[8,256,1024]{2,1,0:T(8,128)(2,1)S(1)}) custom-call(bf16[256,1024]{1,0:T(8,128)(2,1)} %bitcast.8, bf16[2,32,1024]{2,1,0:T(8,128)(2,1)} %bitcast.10, bf16[2,32,1024]{2,1,0:T(8,128)(2,1)} %bitcast.11, bf16[256,1024]{1,0:T(8,128)(2,1)} %bitcast.9, ...), custom_call_target="tpu_custom_call" | custom-call | tf_op jit(solution)/shard_map/gather_products/pallas_call | solution.py:318
  70.9 2.4 %finish.1 = f32[1024,1024]{1,0:T(8,128)} custom-call(f32[1024,1024]{1,0:T(8,128)S(1)} %get-tuple-element.9.base, f32[1024,1024]{1,0:T(8,128)S(1)} %get-tuple-element.10.inv, bf16[1024,768]{1,0:T(8,128)(2,1)S(1)} %get-tuple-element.11.wt, bf16[8,256,1024]{2,1,0:T(8,128)(2,1)S(1)} %get-tuple-element.12.rmt), custom_call_target="tpu_custom_call" | custom-call | tf_op jit(solution)/shard_map/finish/pallas_call | solution.py:346

commit v6 on v5

--- a/solution.py
+++ b/solution.py
@@ -257,15 +257,15 @@
     x_got_forward(1)
     x_got_forward(2)
     share(2)
-    got_share(2)
-    loop(4, lambda n: mix_right(2, n - 1))
-    loop(3, lambda n: mix_right(n - 1, 2))
-    mirror_slots([(0, True)], first=True)
     ring_got("y", A0, True, "-")
     ring_got_forward("y", A0, True, "+")
     ring_got("p", A0, False, "-")
     ring_got_forward("p", A0, False, "+")
     loop(8, lambda n: mix_left(0, n))
+    got_share(2)
+    loop(4, lambda n: mix_right(2, n - 1))
+    loop(3, lambda n: mix_right(n - 1, 2))
+    mirror_slots([(0, True)], first=True)
     ring_got("y", A1, True, "+")
     ring_got_forward("y", A1, True, "-")
     ring_got("p", A1, False, "+")

time: 74.5 us -> 74.1 us (level)
  no operation moved by 1% of the time
where the time goes in v6:
time: 74.1 us; the launch traced here: 73.1 us
  Pallas kernels  71.8 us (97%)
  between operations  1.3 us (2%)
    pallas_call x1, Pallas kernels, body(): pl.pallas_call(gather_kernel, out_shape=[jax.ShapeDtypeStruct((1024, 1024...  69.4 us
    pallas_call x1, Pallas kernels, body(): pl.pallas_call(finish_kernel, out_shape=jax.ShapeDtypeStruct((1024, 1024)...  2.36 us

profile of v6, /device:TPU:1, one launch (start us, length us, event | category | flops | bytes accessed | tf_op | source)
XLA Modules:
  0.0 73.1 jit_solution(9519994057105417232)
XLA Ops:
  1.3 69.4 %gather_products.1 = (f32[1024,1024]{1,0:T(8,128)S(1)}, f32[1024,1024]{1,0:T(8,128)S(1)}, bf16[1024,768]{1,0:T(8,128)(2,1)S(1)}, bf16[8,256,1024]{2,1,0:T(8,128)(2,1)S(1)}) custom-call(bf16[256,1024]{1,0:T(8,128)(2,1)} %bitcast.8, bf16[2,32,1024]{2,1,0:T(8,128)(2,1)} %bitcast.10, bf16[2,32,1024]{2,1,0:T(8,128)(2,1)} %bitcast.11, bf16[256,1024]{1,0:T(8,128)(2,1)} %bitcast.9, ...), custom_call_target="tpu_custom_call" | custom-call | tf_op jit(solution)/shard_map/gather_products/pallas_call | solution.py:318
  70.7 2.4 %finish.1 = f32[1024,1024]{1,0:T(8,128)} custom-call(f32[1024,1024]{1,0:T(8,128)S(1)} %get-tuple-element.9.base, f32[1024,1024]{1,0:T(8,128)S(1)} %get-tuple-element.10.inv, bf16[1024,768]{1,0:T(8,128)(2,1)S(1)} %get-tuple-element.11.wt, bf16[8,256,1024]{2,1,0:T(8,128)(2,1)S(1)} %get-tuple-element.12.rmt), custom_call_target="tpu_custom_call" | custom-call | tf_op jit(solution)/shard_map/finish/pallas_call | solution.py:346
